TPU v7x, 32 devices: a whole 2x2x4 slice. The times are simulated.
32 devices in a mesh: row: 4 (over y, core), col: 8 (over z, x).
Axes of the slice: x: 2, y: 2, z: 4, core: 2. Of those that a mesh axis runs over, the one named last changes fastest.
Arguments:
- panel: bfloat16 [128, 512, 128], P('row', 'col'), may hold values from -1.296875 to 1.296875
- bases: bfloat16 [128, 1024, 128], P('row', 'col'), may hold values from -0.5 to 0.5
- pivots: float32 [512], P('col'), may hold values from 0.25 to 4
- ranks: int32 [128], P('row'), may hold values from 32 to 128
- pairs: int32 [128, 2], P('row'), may hold values from 0 to 127, as said below
- targets: bfloat16 [128, 1024, 1024], P('row', 'col'), may hold values from -6 to 6
Outputs:
- updated: bfloat16 [128, 1024, 1024], P('row', 'col')
Inputs may be any that keep to these rules, and one draw needn't show every extreme that they name: Row p has column tile j = pairs[p, 1] in [b * 32, (b + 1) * 32) with b = p // 32, and row tile i = pairs[p, 0] with j <= i.
All inputs are finite; a program needn't handle non-finite values.
Results may differ from a plain program's by a relative error of at most 0.0056.
Values may be sent and summed in bfloat16 or wider, within the bound.
No kernel may reach another device: no remote copies, remote signals or barrier semaphores. Data moves between devices by JAX's collectives and lax.ppermute only.
A program may use at most 128 MiB of HBM per device.

v0:
```python
import jax
import jax.numpy as jnp
from jax import lax
from jax.sharding import PartitionSpec as P


def shards(panel, bases, pivots, ranks, pairs, targets):
    keep = lax.broadcasted_iota(jnp.int32, (1, 1, panel.shape[2]), 2) < ranks[:, None, None]
    masked = jnp.where(keep, panel, jnp.zeros_like(panel))
    scaled = (masked.astype(jnp.float32) * pivots[None, :, None]).astype(jnp.bfloat16)
    every_scaled, every_panel = (
        lax.all_gather(scaled, "row", axis=0, tiled=True),
        lax.all_gather(masked, "row", axis=0, tiled=True),
    )
    row_tile = pairs[:, 0]
    col_tile = pairs[:, 1]
    partial_value = jnp.einsum(
        "pwa,pwb->pab",
        every_scaled[row_tile],
        every_panel[col_tile],
        preferred_element_type=jnp.float32,
    )
    cores_b = lax.psum(partial_value, "col").astype(jnp.bfloat16)
    every_rows = lax.all_gather(bases, "row", axis=0, tiled=True)
    left = every_rows[row_tile]
    local_col = col_tile - lax.axis_index("row") * bases.shape[0]
    whole_bases = lax.all_gather(bases, "col", axis=1, tiled=True)
    factor = jnp.einsum(
        "pab,pkb->pak", cores_b, whole_bases[local_col], preferred_element_type=jnp.float32
    ).astype(jnp.bfloat16)
    update = jnp.einsum("pka,pac->pkc", left, factor, preferred_element_type=jnp.float32)
    return (targets.astype(jnp.float32) - update).astype(jnp.bfloat16)


def solution(mesh):
    return jax.shard_map(
        shards,
        mesh=mesh,
        in_specs=(
            P("row", "col", None),
            P("row", "col", None),
            P("col"),
            P("row"),
            P("row", None),
            P("row", "col", None),
        ),
        out_specs=P("row", "col", None),
        check_vma=False,
    )
```

profile of v0, /device:TPU:0, one launch (start us, length us, event | category | flops | bytes accessed | tf_op | source)
XLA Modules:
  0.0 268.9 jit_solution(14847740714883652572)
XLA Ops:
  6.5 0.0 all-gather.7.cloned.1.call-start
  6.5 0.7 iota_compare_fusion
  7.3 2.3 multiply_convert_fusion
  9.6 0.0 all-gather.7.cloned.1.call-update
  9.6 0.0 all-gather.9.cloned.1.call-start
  9.7 0.7 all-gather.9.cloned.1.call-update
  10.4 0.0 all-gather.5.cloned.1.call-start
  10.4 0.7 all-gather.5.cloned.1.call-update
  11.1 0.0 all-gather.11.cloned.1.call-start
  11.2 0.5 all-gather.11.cloned.1.call-update
  11.7 0.8 fusion.6
  12.5 22.6 %all-gather.7.cloned.1.call-done = bf16[128,64,128]{2,1,0:T(8,128)(2,1)} async-done(((bf16[32,64,128]{2,1,0:T(8,128)(2,1)}), bf16[128,64,128]{2,1,0:T(8,128)(2,1)}) %all-gather.7.cloned.1.call-update) | async-done | bytes 2097168 | tf_op jit(solution)/shard_map/all_gather | solution.py:12
  35.1 2.2 gather_fusion.1
  37.3 21.9 %all-gather.9.cloned.1.call-done = bf16[128,64,128]{2,1,0:T(8,128)(2,1)} async-done(((bf16[32,64,128]{2,1,0:T(8,128)(2,1)}), bf16[128,64,128]{2,1,0:T(8,128)(2,1)}) %all-gather.9.cloned.1.call-update) | async-done | bytes 2097168 | tf_op jit(solution)/shard_map/all_gather | solution.py:13
  59.2 2.2 gather_fusion.2
  61.5 0.5 fusion.8
  62.0 105.9 %all-reduce.1 = bf16[32,128,128]{2,1,0:T(8,128)(2,1)S(1)} all-reduce(f32[32,128,128]{2,1,0:T(8,128)S(1)} %fusion.8), channel_id=1, replica_groups=mesh['row'=4,'col'=8] {'col'}, use_global_device_ids=true, to_apply=%region_0.1 | all-reduce | flops 524288 | bytes 3145728 | tf_op jit(solution)/shard_map/psum | solution.py:23
  167.9 0.0 all-gather.5.cloned.1.call-done
  167.9 2.9 %gather_fusion = bf16[32,128,128]{2,1,0:T(8,128)(2,1)S(1)} fusion(bf16[128,128,128]{2,1,0:T(8,128)(2,1)} %all-gather.5.cloned.1.call-done, s32[1024]{0:T(1024)S(1)} %pad_clamp_fusion.2), kind=kCustom, calls=%fused_computation | custom fusion | bytes 2097280 | tf_op jit(solution)/shard_map/gather | solution.py:25
  170.8 72.9 %all-gather.11.cloned.1.call-done = bf16[32,1024,128]{2,1,0:T(8,128)(2,1)} async-done(((bf16[32,128,128]{2,1,0:T(8,128)(2,1)}), bf16[32,1024,128]{2,1,0:T(8,128)(2,1)}) %all-gather.11.cloned.1.call-update) | async-done | bytes 8388624 | tf_op jit(solution)/shard_map/all_gather | solution.py:27
  243.8 8.4 %gather_fusion.3 = bf16[32,1024,128]{2,1,0:T(8,128)(2,1)} fusion(bf16[32,1024,128]{2,1,0:T(8,128)(2,1)} %all-gather.11.cloned.1.call-done, s32[1024]{0:T(1024)S(1)} %pad_clamp_fusion), kind=kCustom, calls=%fused_computation.3 | custom fusion | bytes 16777344 | tf_op jit(solution)/shard_map/gather | solution.py:29
  252.2 10.2 %subtract_convert_fusion = bf16[32,128,1024]{2,1,0:T(8,128)(2,1)} fusion(bf16[32,128,1024]{2,1,0:T(8,128)(2,1)} %param.11, bf16[32,128,128]{2,1,0:T(8,128)(2,1)S(1)} %gather_fusion, bf16[32,1024,128]{2,1,0:T(8,128)(2,1)} %gather_fusion.3, bf16[32,128,128]{2,1,0:T(8,128)(2,1)S(1)} %all-reduce.1), kind=kOutput, calls=%fused_computation.4 | convolution fusion | flops 2164260864 | bytes 27262976 | tf_op jit(solution)/shard_map/pka,pac->pkc/dot_general | solution.py:31
  (3 shorter events, 0.0 us)
Async XLA Ops:
  6.5 28.5 %all-gather.7.cloned.1.call-start = ((), (), s32[]{:S(2)}) async-start(), calls=%async_computation.1 | async-start | bytes 2621440 | tf_op jit(solution)/shard_map/all_gather | solution.py:12
  9.6 49.6 %all-gather.9.cloned.1.call-start = ((), (), s32[]{:S(2)}) async-start(), calls=%async_computation.2 | async-start | bytes 2621440 | tf_op jit(solution)/shard_map/all_gather | solution.py:13
  10.4 157.5 %all-gather.5.cloned.1.call-start = ((), (), s32[]{:S(2)}) async-start(), calls=%async_computation | async-start | bytes 5242880 | tf_op jit(solution)/shard_map/all_gather | solution.py:24
  11.1 232.6 %all-gather.11.cloned.1.call-start = ((), (), s32[]{:S(2)}) async-start(), calls=%async_computation.3 | async-start | bytes 9437184 | tf_op jit(solution)/shard_map/all_gather | solution.py:27
Sparse Core Ops, SparseCore 0:
  9.8 25.2 all-gather.6
  36.6 22.5 all-gather.8
  60.8 34.4 all-gather.4
  97.3 146.3 all-gather.10
where the time goes:
time: 269 us
  waiting for transfers between devices  119 us (44%)
  blocking collectives  106 us (39%)
  local copies, waits for them, and re-layouts  15.8 us (6%)
  between operations  13.2 us (5%)
  matrix products  10.7 us (4%)
  other arithmetic  3.85 us (1%)
    psum x1, blocking collectives, shards(): cores_b = lax.psum(partial_value, 'col').astype(jnp.bfloat16)  106 us
    all_gather x1, waiting for transfers between devices, shards(): whole_bases = lax.all_gather(bases, 'col', axis=1, tiled=True)  72.9 us
    all_gather x1, waiting for transfers between devices, shards(): lax.all_gather(scaled, 'row', axis=0, tiled=True)  22.6 us
    all_gather x1, waiting for transfers between devices, shards(): lax.all_gather(masked, 'row', axis=0, tiled=True)  21.9 us
    dot_general x1, matrix products, shards(): jnp.einsum('pka,pac->pkc', left, factor, preferred_element_type=jnp.float32)  10.2 us
    gather x1, local copies, waits for them, and re-layouts, shards(): whole_bases[local_col]  8.39 us
  transfers between devices with their start and end apart: 4, of which 3 were waited for; matrix products, arithmetic and copies ran while one was open for 3% of the time, Pallas kernels for 0%

commit v1 on v0

v1 whole, which is shorter than its diff:
```python
import functools

import jax
import jax.numpy as jnp
from jax import lax
from jax.experimental import pallas as pl
from jax.experimental.pallas import tpu as pltpu
from jax.sharding import PartitionSpec as P

VMEM = pltpu.VMEM
SMEM = pltpu.SMEM
SUBS = 2


def cycle(size):
    wide = 1
    while (wide * 2) ** 2 <= size:
        wide *= 2
    deep = size // wide
    walk = [z * wide for z in range(deep)]
    for z in reversed(range(deep)):
        across = list(range(1, wide))
        if (deep - 1 - z) % 2 == 1:
            across.reverse()
        walk += [z * wide + x for x in across]
    return walk


def select_kernel(index_ref, *refs):
    out_ref, bufs = refs[-1], refs[:-1]
    tiles = bufs[0].shape[0]

    def body(p, carry):
        where = index_ref[p]
        for s, buf in enumerate(bufs):
            @pl.when(where // tiles == s)
            def _():
                out_ref[p] = buf[where % tiles]
        return carry

    lax.fori_loop(0, out_ref.shape[0], body, 0)


def select(index, *bufs):
    shape = (index.shape[0],) + bufs[0].shape[1:]
    size = shape[0] * shape[1] * shape[2] * 2
    return pl.pallas_call(
        select_kernel,
        out_shape=jax.ShapeDtypeStruct(shape, bufs[0].dtype),
        in_specs=[pl.BlockSpec(memory_space=SMEM)] + [pl.BlockSpec(memory_space=VMEM)] * len(bufs),
        out_specs=pl.BlockSpec(memory_space=VMEM),
        name="select",
        cost_estimate=pl.CostEstimate(flops=10_000_000, bytes_accessed=2 * size, transcendentals=0),
    )(index, *bufs)


def core_kernel(scaled_ref, masked_ref, out_ref):
    parts, pairs = scaled_ref.shape[:2]
    for p in range(pairs):
        total = jnp.zeros(out_ref.shape[1:], jnp.float32)
        for c in range(parts):
            total += lax.dot_general(
                scaled_ref[c, p], masked_ref[c, p], (((0,), (0,)), ((), ())),
                preferred_element_type=jnp.float32,
            )
        out_ref[p] = total.astype(out_ref.dtype)


def make_cores(scaled, masked):
    parts, pairs, rows, rank = scaled.shape
    return pl.pallas_call(
        core_kernel,
        out_shape=jax.ShapeDtypeStruct((pairs, rank, rank), jnp.bfloat16),
        in_specs=[pl.BlockSpec(memory_space=VMEM)] * 2,
        out_specs=pl.BlockSpec(memory_space=VMEM),
        name="cores",
        cost_estimate=pl.CostEstimate(
            flops=2 * parts * pairs * rows * rank * rank,
            bytes_accessed=4 * parts * pairs * rows * rank, transcendentals=0,
        ),
    )(scaled, masked)


def final_kernel(steps, chains, lefts, row_ref, col_ref, source_ref, targets_ref, cores_ref, own_ref, *refs):
    out_ref, left_ref, whole_ref = refs[-3:]
    left_bufs, ring = refs[:lefts], refs[lefts:-3]
    tiles = own_ref.shape[0]
    rows = own_ref.shape[1]
    group = tiles // chains
    p = pl.program_id(0)

    @pl.when(p == 0)
    def _():
        for g in range(chains):
            for s in range(steps + 1):
                at = pl.ds(pl.multiple_of(source_ref[g % 2, s] * rows, rows), rows)
                part = own_ref[g * group:(g + 1) * group] if s == 0 else ring[g * steps + s - 1][...]
                whole_ref[g * group:(g + 1) * group, at] = part

    where = row_ref[p]
    for s in range(lefts):
        @pl.when(where // tiles == s)
        def _():
            left_ref[...] = jnp.dot(
                left_bufs[s][where % tiles], cores_ref[p], preferred_element_type=jnp.float32
            ).astype(left_ref.dtype)
    block = whole_ref[col_ref[p]]
    update = lax.dot_general(
        left_ref[...], block, (((1,), (1,)), ((), ())), preferred_element_type=jnp.float32
    )
    out_ref[0] = (targets_ref[0].astype(jnp.float32) - update).astype(out_ref.dtype)


def finish(row_index, col_index, sources, targets, cores, own, left_bufs, ring, chains, steps):
    pairs, rows, width = targets.shape
    rank = cores.shape[1]
    block = pl.BlockSpec((1, rows, width), lambda p: (p, 0, 0))
    return pl.pallas_call(
        functools.partial(final_kernel, steps, chains, len(left_bufs)),
        grid=(pairs,),
        out_shape=jax.ShapeDtypeStruct(targets.shape, targets.dtype),
        in_specs=[pl.BlockSpec(memory_space=SMEM)] * 3 + [block]
        + [pl.BlockSpec(memory_space=VMEM)] * (2 + len(left_bufs) + len(ring)),
        out_specs=block,
        scratch_shapes=[VMEM((rows, rank), jnp.bfloat16), VMEM((own.shape[0], width, rank), jnp.bfloat16)],
        name="finish",
        cost_estimate=pl.CostEstimate(
            flops=2 * pairs * rows * rank * (width + rank),
            bytes_accessed=4 * pairs * rows * width, transcendentals=0,
        ),
    )(row_index, col_index, sources, targets, cores, own, *left_bufs, *ring)


def spread_rows(block, n_row):
    swap = [(r, r ^ 1) for r in range(n_row)]
    got = [block, lax.ppermute(block, "row", swap)]
    for k in range(1, n_row // 2):
        shifted = lax.ppermute(block, "row", [(r, r - 2 * k) for r in range(2 * k, n_row)])
        got += [shifted, lax.ppermute(shifted, "row", swap)]
    return got


def shards(n_row, n_col, panel, bases, pivots, ranks, pairs, targets):
    tiles = panel.shape[0]
    n_pairs = pairs.shape[0]
    per = n_pairs // n_col
    r = lax.axis_index("row")
    c = lax.axis_index("col")
    row_tile, col_tile = pairs[:, 0], pairs[:, 1]
    block = row_tile // tiles - (r // 2) * 2
    slot = (block // 2) * 2 + ((block % 2) != (r % 2)).astype(jnp.int32)
    row_index = slot * tiles + row_tile % tiles
    col_index = col_tile - r * tiles

    keep = lax.broadcasted_iota(jnp.int32, (1, 1, panel.shape[2]), 2) < ranks[:, None, None]
    masked = jnp.where(keep, panel, jnp.zeros_like(panel))
    scaled = (masked.astype(jnp.float32) * pivots[None, :, None]).astype(jnp.bfloat16)

    walk = cycle(n_col)
    steps = n_col - 1
    forward = [(walk[k], walk[(k + 1) % n_col]) for k in range(n_col)]
    backward = [(b, a) for a, b in forward]
    chains = 2 * SUBS
    group = tiles // chains
    ring = []
    for g in range(chains):
        held = bases[g * group:(g + 1) * group]
        for _ in range(steps):
            held = lax.ppermute(held, "col", (forward, backward)[g % 2])
            ring.append(held)
    table = jnp.array(
        [[[walk[(walk.index(me) + sign * s) % n_col] for s in range(n_col)] for sign in (-1, 1)]
         for me in range(n_col)], jnp.int32)
    sources = table[c]

    def exchange(x):
        return lax.all_to_all(x.reshape((n_col, per) + x.shape[1:]), "col", 0, 0)

    masked_parts = exchange(select(col_index, masked))
    scaled_parts = exchange(select(row_index, *spread_rows(scaled, n_row)))
    own_cores = make_cores(scaled_parts, masked_parts)
    cores = lax.all_to_all(
        jnp.broadcast_to(own_cores[None], (n_col,) + own_cores.shape), "col", 0, 0
    ).reshape((n_pairs,) + own_cores.shape[1:])
    left_bufs = spread_rows(bases, n_row)
    return finish(row_index, col_index, sources, targets, cores, bases, left_bufs, ring, chains, steps)


def solution(mesh):
    return jax.shard_map(
        functools.partial(shards, mesh.shape["row"], mesh.shape["col"]),
        mesh=mesh,
        in_specs=(
            P("row", "col", None),
            P("row", "col", None),
            P("col"),
            P("row"),
            P("row", None),
            P("row", "col", None),
        ),
        out_specs=P("row", "col", None),
        check_vma=False,
    )
```

time: 269 us -> 187 us (0.70); the launches traced: 269 us -> 184 us
  blocking collectives: 106 us -> 0 us
  starting transfers between devices: 0.12 us -> 72.7 us
  waiting for transfers between devices: 119 us -> 60.8 us
  Pallas kernels: 0 us -> 38 us
  between operations: 13.2 us -> 0.2 us
  matrix products: 10.7 us -> 0 us
  local copies, waits for them, and re-layouts: 15.8 us -> 7.13 us
    all_gather x4 -> x0, waiting for transfers between devices: 117 us -> none  [the longest x1 72.9 us: shards(): whole_bases = lax.all_gather(bases, 'col', axis=1, tiled=True)]
    psum x1 -> x0, blocking collectives: 106 us -> none  [shards(): cores_b = lax.psum(partial_value, 'col').astype(jnp.bfloat16)]
    ppermute x0 -> x34, starting transfers between devices: none -> 58.2 us  [the longest x28 55.6 us: shards(): held = lax.ppermute(held, 'col', (forward, backward)[g % 2])]
    ppermute x0 -> x34, waiting for transfers between devices: none -> 55.8 us  [the longest x28 51.1 us: shards(): held = lax.ppermute(held, 'col', (forward, backward)[g % 2])]
    pallas_call x0 -> x4, Pallas kernels: none -> 38 us  [the longest x1 29.6 us: finish(): pl.pallas_call(functools.partial(final_kernel, steps, chains, len(left_bu...]
    gather x4 -> x0, local copies, waits for them, and re-layouts: 15.8 us -> none  [the longest x1 8.39 us: shards(): whole_bases[local_col]]
    all_to_all x0 -> x3, starting transfers between devices: none -> 14.5 us  [the longest x2 10.9 us: exchange(): return lax.all_to_all(x.reshape((n_col, per) + x.shape[1:]), 'col', 0, 0)]
    dot_general x2 -> x0, matrix products: 10.7 us -> none  [the longest x1 10.2 us: shards(): jnp.einsum('pka,pac->pkc', left, factor, preferred_element_type=jnp.float32)]
  transfers between devices with their start and end apart: 4 -> 37, of which waited for: 3 -> 22; matrix products, arithmetic and copies ran while one was open for 3% -> 4% of each run, Pallas kernels for 0% -> 5%
where the time goes in v1:
time: 187 us; the launch traced here: 184 us
  starting transfers between devices  72.7 us (39%)
  waiting for transfers between devices  60.8 us (33%)
  Pallas kernels  38 us (20%)
  local copies, waits for them, and re-layouts  7.13 us (4%)
  other arithmetic  5.39 us (3%)
    ppermute x28, starting transfers between devices, shards(): held = lax.ppermute(held, 'col', (forward, backward)[g % 2])  55.6 us
    ppermute x28, waiting for transfers between devices, shards(): held = lax.ppermute(held, 'col', (forward, backward)[g % 2])  51.1 us
    pallas_call x1, Pallas kernels, finish(): pl.pallas_call(functools.partial(final_kernel, steps, chains, len(left_bu...  29.6 us
    all_to_all x2, starting transfers between devices, exchange(): return lax.all_to_all(x.reshape((n_col, per) + x.shape[1:]), 'col', 0, 0)  10.9 us
    pallas_call x2, Pallas kernels, select(): pl.pallas_call(select_kernel, out_shape=jax.ShapeDtypeStruct(shape, bufs[...  6.03 us
    all_to_all x2, waiting for transfers between devices, exchange(): return lax.all_to_all(x.reshape((n_col, per) + x.shape[1:]), 'col', 0, 0)  5.04 us
    ppermute x2, waiting for transfers between devices, spread_rows(): lax.ppermute(block, 'row', [(r, r - 2 * k) for r in range(2 * k, n_row)])  3.88 us
  transfers between devices with their start and end apart: 37, of which 22 were waited for; matrix products, arithmetic and copies ran while one was open for 4% of the time, Pallas kernels for 5%

profile of v1, /device:TPU:0, one launch (start us, length us, event | category | flops | bytes accessed | tf_op | source)
XLA Modules:
  0.0 184.2 jit_solution(5839981533025973820)
XLA Ops:
  0.8 2.2 %multiply_convert_fusion = (bf16[32,64,128]{2,1,0:T(8,128)(2,1)S(1)}, bf16[32,64,128]{2,1,0:T(8,128)(2,1)}) fusion(f32[64]{0:T(128)} %param.9, bf16[32,64,128]{2,1,0:T(8,128)(2,1)} %param.7, pred[32,128]{1,0:T(8,128)(4,1)S(1)} %iota_compare_fusion), kind=kLoop, calls=%fused_computation | loop fusion | flops 1048576 | bytes 1577216 | tf_op jit(solution)/shard_map/convert_element_type | solution.py:157
  3.0 1.3 collective-permute-start.1
  4.3 1.2 subtract_bitcast_fusion.index_ref.col_ref
  5.5 2.5 %select.21 = bf16[32,64,128]{2,1,0:T(8,128)(2,1)} custom-call(s32[32]{0:T(128)} %subtract_bitcast_fusion.index_ref.col_ref, bf16[32,64,128]{2,1,0:T(8,128)(2,1)} %get-tuple-element.6.refs_0_), custom_call_target="tpu_custom_call" | custom-call | flops 10000000 | bytes 1048576 | tf_op jit(solution)/shard_map/select/pallas_call | solution.py:47
  8.0 7.3 %all-to-all-start.1 = ((bf16[8,4,64,128]{3,2,1,0:T(8,128)(2,1)}), bf16[8,4,64,128]{3,2,1,0:T(8,128)(2,1)S(1)}, u32[]{:S(2)}, u32[]{:S(2)}) async-start(bf16[8,4,64,128]{3,2,1,0:T(8,128)(2,1)} %bitcast.21), calls=%async_computation.1 | async-start | bytes 1048576 | tf_op jit(solution)/shard_map/all_to_all | solution.py:177
  15.3 3.9 %collective-permute-done.1.refs_2_ = bf16[32,64,128]{2,1,0:T(8,128)(2,1)S(1)} collective-permute-done((bf16[32,64,128]{2,1,0:T(8,128)(2,1)S(1)}, bf16[32,64,128]{2,1,0:T(8,128)(2,1)S(1)}, u32[]{:S(2)}, u32[]{:S(2)}) %collective-permute-start.1) | collective-permute-done | bytes 524320 | tf_op jit(solution)/shard_map/ppermute | solution.py:138
  19.2 1.2 fusion.index_ref.row_ref
  21.2 3.5 %select.20 = bf16[32,64,128]{2,1,0:T(8,128)(2,1)} custom-call(s32[32]{0:T(128)} %fusion.index_ref.row_ref, bf16[32,64,128]{2,1,0:T(8,128)(2,1)} %copy-done.4, bf16[32,64,128]{2,1,0:T(8,128)(2,1)} %copy-done.7, bf16[32,64,128]{2,1,0:T(8,128)(2,1)} %copy-done.6, bf16[32,64,128]{2,1,0:T(8,128)(2,1)} %collective-permute-done.2.refs_3_), custom_call_target="tpu_custom_call" | custom-call | flops 10000000 | bytes 1048576 | tf_op jit(solution)/shard_map/select/pallas_call | solution.py:47
  24.7 5.0 %all-to-all-done.1.masked_ref = bf16[8,4,64,128]{3,2,1,0:T(8,128)(2,1)S(1)} async-done(((bf16[8,4,64,128]{3,2,1,0:T(8,128)(2,1)}), bf16[8,4,64,128]{3,2,1,0:T(8,128)(2,1)S(1)}, u32[]{:S(2)}, u32[]{:S(2)}) %all-to-all-start.1) | async-done | bytes 524320 | tf_op jit(solution)/shard_map/all_to_all | solution.py:177
  29.8 3.6 %all-to-all-start = ((bf16[8,4,64,128]{3,2,1,0:T(8,128)(2,1)}), bf16[8,4,64,128]{3,2,1,0:T(8,128)(2,1)S(1)}, u32[]{:S(2)}, u32[]{:S(2)}) async-start(bf16[8,4,64,128]{3,2,1,0:T(8,128)(2,1)} %bitcast.22), calls=%async_computation | async-start | bytes 1048576 | tf_op jit(solution)/shard_map/all_to_all | solution.py:177
  33.4 1.3 fusion.2
  34.7 2.1 %collective-permute-start.27 = (bf16[8,128,128]{2,1,0:T(8,128)(2,1)S(1)}, bf16[8,128,128]{2,1,0:T(8,128)(2,1)S(1)}, u32[]{:S(2)}, u32[]{:S(2)}) collective-permute-start(bf16[8,128,128]{2,1,0:T(8,128)(2,1)S(1)} %get-tuple-element.7), channel_id=1, source_target_pairs={{2,0},{4,2},{6,4},{7,6},{5,7},{3,5},{1,3},{0,1},{10,8},{12,10},{14... | collective-permute-start | bytes 786440 | tf_op jit(solution)/shard_map/ppermute | solution.py:169
  36.9 2.0 %collective-permute-start.13 = (bf16[8,128,128]{2,1,0:T(8,128)(2,1)S(1)}, bf16[8,128,128]{2,1,0:T(8,128)(2,1)}, u32[]{:S(2)}, u32[]{:S(2)}) collective-permute-start(bf16[8,128,128]{2,1,0:T(8,128)(2,1)S(1)} %get-tuple-element.9), channel_id=1, source_target_pairs={{2,0},{4,2},{6,4},{7,6},{5,7},{3,5},{1,3},{0,1},{10,8},{12,10},{14... | collective-permute-start | bytes 786440 | tf_op jit(solution)/shard_map/ppermute | solution.py:169
  38.9 1.3 collective-permute-start.4
  40.2 11.1 %collective-permute-done.27.refs_25_ = bf16[8,128,128]{2,1,0:T(8,128)(2,1)S(1)} collective-permute-done((bf16[8,128,128]{2,1,0:T(8,128)(2,1)S(1)}, bf16[8,128,128]{2,1,0:T(8,128)(2,1)S(1)}, u32[]{:S(2)}, u32[]{:S(2)}) %collective-permute-start.27) | collective-permute-done | bytes 262176 | tf_op jit(solution)/shard_map/ppermute | solution.py:169
  51.2 1.3 collective-permute-start.28
  52.6 3.2 %collective-permute-done.13.refs_11_ = bf16[8,128,128]{2,1,0:T(8,128)(2,1)} collective-permute-done((bf16[8,128,128]{2,1,0:T(8,128)(2,1)S(1)}, bf16[8,128,128]{2,1,0:T(8,128)(2,1)}, u32[]{:S(2)}, u32[]{:S(2)}) %collective-permute-start.13) | collective-permute-done | bytes 262176 | tf_op jit(solution)/shard_map/ppermute | solution.py:169
  55.7 5.5 %collective-permute-start.21 = (bf16[8,128,128]{2,1,0:T(8,128)(2,1)}, bf16[8,128,128]{2,1,0:T(8,128)(2,1)}, u32[]{:S(2)}, u32[]{:S(2)}) collective-permute-start(bf16[8,128,128]{2,1,0:T(8,128)(2,1)} %collective-permute-done.20.refs_18_), channel_id=1, source_target_pairs={{0,2},{2,4},{4,6},{6,7},{7,5},{5,3},{3,1},{1,0},{8,10},{10,12},{12... | collective-permute-start | bytes 786440 | tf_op jit(solution)/shard_map/ppermute | solution.py:169
  62.7 2.3 %cores.1 = bf16[4,128,128]{2,1,0:T(8,128)(2,1)} custom-call(bf16[8,4,64,128]{3,2,1,0:T(8,128)(2,1)} %copy-done.3, bf16[8,4,64,128]{3,2,1,0:T(8,128)(2,1)} %copy-done.2), custom_call_target="tpu_custom_call" | custom-call | flops 67108864 | bytes 1048576 | tf_op jit(solution)/shard_map/cores/pallas_call | solution.py:71
  65.1 2.1 %broadcast_in_dim.21 = bf16[8,4,128,128]{3,2,1,0:T(8,128)(2,1)} broadcast(bf16[4,128,128]{2,1,0:T(8,128)(2,1)} %cores.1), dimensions={1,2,3} | broadcast | bytes 1179648 | tf_op jit(solution)/shard_map/broadcast_in_dim | solution.py:183
  67.2 3.6 %all-to-all-start.2 = ((bf16[8,4,128,128]{3,2,1,0:T(8,128)(2,1)}), bf16[8,4,128,128]{3,2,1,0:T(8,128)(2,1)S(1)}, u32[]{:S(2)}, u32[]{:S(2)}) async-start(bf16[8,4,128,128]{3,2,1,0:T(8,128)(2,1)} %broadcast_in_dim.21), calls=%async_computation.2 | async-start | bytes 2097152 | tf_op jit(solution)/shard_map/all_to_all | solution.py:182
  70.8 2.0 %collective-permute-start.7 = (bf16[8,128,128]{2,1,0:T(8,128)(2,1)}, bf16[8,128,128]{2,1,0:T(8,128)(2,1)S(1)}, u32[]{:S(2)}, u32[]{:S(2)}) collective-permute-start(bf16[8,128,128]{2,1,0:T(8,128)(2,1)} %copy-done.9), channel_id=1, source_target_pairs={{0,2},{2,4},{4,6},{6,7},{7,5},{5,3},{3,1},{1,0},{8,10},{10,12},{12... | collective-permute-start | bytes 786440 | tf_op jit(solution)/shard_map/ppermute | solution.py:169
  72.8 2.0 %collective-permute-start.22 = (bf16[8,128,128]{2,1,0:T(8,128)(2,1)}, bf16[8,128,128]{2,1,0:T(8,128)(2,1)S(1)}, u32[]{:S(2)}, u32[]{:S(2)}) collective-permute-start(bf16[8,128,128]{2,1,0:T(8,128)(2,1)} %collective-permute-done.21.refs_19_), channel_id=1, source_target_pairs={{0,2},{2,4},{4,6},{6,7},{7,5},{5,3},{3,1},{1,0},{8,10},{10,12},{12... | collective-permute-start | bytes 786440 | tf_op jit(solution)/shard_map/ppermute | solution.py:169
  74.8 19.8 %collective-permute-done.7.refs_5_ = bf16[8,128,128]{2,1,0:T(8,128)(2,1)S(1)} collective-permute-done((bf16[8,128,128]{2,1,0:T(8,128)(2,1)}, bf16[8,128,128]{2,1,0:T(8,128)(2,1)S(1)}, u32[]{:S(2)}, u32[]{:S(2)}) %collective-permute-start.7) | collective-permute-done | bytes 262176 | tf_op jit(solution)/shard_map/ppermute | solution.py:169
  94.6 2.1 %collective-permute-start.15 = (bf16[8,128,128]{2,1,0:T(8,128)(2,1)}, bf16[8,128,128]{2,1,0:T(8,128)(2,1)S(1)}, u32[]{:S(2)}, u32[]{:S(2)}) collective-permute-start(bf16[8,128,128]{2,1,0:T(8,128)(2,1)} %collective-permute-done.14.refs_12_), channel_id=1, source_target_pairs={{2,0},{4,2},{6,4},{7,6},{5,7},{3,5},{1,3},{0,1},{10,8},{12,10},{14... | collective-permute-start | bytes 786440 | tf_op jit(solution)/shard_map/ppermute | solution.py:169
  96.7 5.3 %collective-permute-start.8 = (bf16[8,128,128]{2,1,0:T(8,128)(2,1)S(1)}, bf16[8,128,128]{2,1,0:T(8,128)(2,1)S(1)}, u32[]{:S(2)}, u32[]{:S(2)}) collective-permute-start(bf16[8,128,128]{2,1,0:T(8,128)(2,1)S(1)} %collective-permute-done.7.refs_5_), channel_id=1, source_target_pairs={{0,2},{2,4},{4,6},{6,7},{7,5},{5,3},{3,1},{1,0},{8,10},{10,12},{12... | collective-permute-start | bytes 786440 | tf_op jit(solution)/shard_map/ppermute | solution.py:169
  102.0 2.3 %collective-permute-start.30 = (bf16[8,128,128]{2,1,0:T(8,128)(2,1)S(1)}, bf16[8,128,128]{2,1,0:T(8,128)(2,1)S(1)}, u32[]{:S(2)}, u32[]{:S(2)}) collective-permute-start(bf16[8,128,128]{2,1,0:T(8,128)(2,1)S(1)} %collective-permute-done.29.refs_27_), channel_id=1, source_target_pairs={{2,0},{4,2},{6,4},{7,6},{5,7},{3,5},{1,3},{0,1},{10,8},{12,10},{14... | collective-permute-start | bytes 786440 | tf_op jit(solution)/shard_map/ppermute | solution.py:169
  104.3 1.5 collective-permute-done.15.refs_13_
  105.8 2.4 %collective-permute-start.23 = (bf16[8,128,128]{2,1,0:T(8,128)(2,1)S(1)}, bf16[8,128,128]{2,1,0:T(8,128)(2,1)S(1)}, u32[]{:S(2)}, u32[]{:S(2)}) collective-permute-start(bf16[8,128,128]{2,1,0:T(8,128)(2,1)S(1)} %collective-permute-done.22.refs_20_), channel_id=1, source_target_pairs={{0,2},{2,4},{4,6},{6,7},{7,5},{5,3},{3,1},{1,0},{8,10},{10,12},{12... | collective-permute-start | bytes 786440 | tf_op jit(solution)/shard_map/ppermute | solution.py:169
  108.6 2.3 %collective-permute-start.16 = (bf16[8,128,128]{2,1,0:T(8,128)(2,1)S(1)}, bf16[8,128,128]{2,1,0:T(8,128)(2,1)S(1)}, u32[]{:S(2)}, u32[]{:S(2)}) collective-permute-start(bf16[8,128,128]{2,1,0:T(8,128)(2,1)S(1)} %collective-permute-done.15.refs_13_), channel_id=1, source_target_pairs={{2,0},{4,2},{6,4},{7,6},{5,7},{3,5},{1,3},{0,1},{10,8},{12,10},{14... | collective-permute-start | bytes 786440 | tf_op jit(solution)/shard_map/ppermute | solution.py:169
  111.5 2.3 %collective-permute-start.9 = (bf16[8,128,128]{2,1,0:T(8,128)(2,1)S(1)}, bf16[8,128,128]{2,1,0:T(8,128)(2,1)S(1)}, u32[]{:S(2)}, u32[]{:S(2)}) collective-permute-start(bf16[8,128,128]{2,1,0:T(8,128)(2,1)S(1)} %collective-permute-done.8.refs_6_), channel_id=1, source_target_pairs={{0,2},{2,4},{4,6},{6,7},{7,5},{5,3},{3,1},{1,0},{8,10},{10,12},{12... | collective-permute-start | bytes 786440 | tf_op jit(solution)/shard_map/ppermute | solution.py:169
  114.2 2.3 %collective-permute-start.31 = (bf16[8,128,128]{2,1,0:T(8,128)(2,1)S(1)}, bf16[8,128,128]{2,1,0:T(8,128)(2,1)S(1)}, u32[]{:S(2)}, u32[]{:S(2)}) collective-permute-start(bf16[8,128,128]{2,1,0:T(8,128)(2,1)S(1)} %collective-permute-done.30.refs_28_), channel_id=1, source_target_pairs={{2,0},{4,2},{6,4},{7,6},{5,7},{3,5},{1,3},{0,1},{10,8},{12,10},{14... | collective-permute-start | bytes 786440 | tf_op jit(solution)/shard_map/ppermute | solution.py:169
  116.8 2.6 %collective-permute-start.24 = (bf16[8,128,128]{2,1,0:T(8,128)(2,1)S(1)}, bf16[8,128,128]{2,1,0:T(8,128)(2,1)S(1)}, u32[]{:S(2)}, u32[]{:S(2)}) collective-permute-start(bf16[8,128,128]{2,1,0:T(8,128)(2,1)S(1)} %collective-permute-done.23.refs_21_), channel_id=1, source_target_pairs={{0,2},{2,4},{4,6},{6,7},{7,5},{5,3},{3,1},{1,0},{8,10},{10,12},{12... | collective-permute-start | bytes 786440 | tf_op jit(solution)/shard_map/ppermute | solution.py:169
  119.8 2.3 %collective-permute-start.17 = (bf16[8,128,128]{2,1,0:T(8,128)(2,1)S(1)}, bf16[8,128,128]{2,1,0:T(8,128)(2,1)S(1)}, u32[]{:S(2)}, u32[]{:S(2)}) collective-permute-start(bf16[8,128,128]{2,1,0:T(8,128)(2,1)S(1)} %collective-permute-done.16.refs_14_), channel_id=1, source_target_pairs={{2,0},{4,2},{6,4},{7,6},{5,7},{3,5},{1,3},{0,1},{10,8},{12,10},{14... | collective-permute-start | bytes 786440 | tf_op jit(solution)/shard_map/ppermute | solution.py:169
  122.1 0.8 collective-permute-start.10
  123.2 3.5 %collective-permute-start.32 = (bf16[8,128,128]{2,1,0:T(8,128)(2,1)S(1)}, bf16[8,128,128]{2,1,0:T(8,128)(2,1)S(1)}, u32[]{:S(2)}, u32[]{:S(2)}) collective-permute-start(bf16[8,128,128]{2,1,0:T(8,128)(2,1)S(1)} %collective-permute-done.31.refs_29_), channel_id=1, source_target_pairs={{2,0},{4,2},{6,4},{7,6},{5,7},{3,5},{1,3},{0,1},{10,8},{12,10},{14... | collective-permute-start | bytes 786440 | tf_op jit(solution)/shard_map/ppermute | solution.py:169
  126.8 1.8 collective-permute-start.25
  128.5 1.5 collective-permute-done.17.refs_15_
  130.1 3.3 %collective-permute-start.18 = (bf16[8,128,128]{2,1,0:T(8,128)(2,1)S(1)}, bf16[8,128,128]{2,1,0:T(8,128)(2,1)S(1)}, u32[]{:S(2)}, u32[]{:S(2)}) collective-permute-start(bf16[8,128,128]{2,1,0:T(8,128)(2,1)S(1)} %collective-permute-done.17.refs_15_), channel_id=1, source_target_pairs={{2,0},{4,2},{6,4},{7,6},{5,7},{3,5},{1,3},{0,1},{10,8},{12,10},{14... | collective-permute-start | bytes 786440 | tf_op jit(solution)/shard_map/ppermute | solution.py:169
  134.1 1.5 collective-permute-done.32.refs_30_
  135.7 3.3 %collective-permute-start.33 = (bf16[8,128,128]{2,1,0:T(8,128)(2,1)S(1)}, bf16[8,128,128]{2,1,0:T(8,128)(2,1)}, u32[]{:S(2)}, u32[]{:S(2)}) collective-permute-start(bf16[8,128,128]{2,1,0:T(8,128)(2,1)S(1)} %collective-permute-done.32.refs_30_), channel_id=1, source_target_pairs={{2,0},{4,2},{6,4},{7,6},{5,7},{3,5},{1,3},{0,1},{10,8},{12,10},{14... | collective-permute-start | bytes 786440 | tf_op jit(solution)/shard_map/ppermute | solution.py:169
  139.8 1.5 collective-permute-done.18.refs_16_
  141.3 3.3 %collective-permute-start.19 = (bf16[8,128,128]{2,1,0:T(8,128)(2,1)S(1)}, bf16[8,128,128]{2,1,0:T(8,128)(2,1)}, u32[]{:S(2)}, u32[]{:S(2)}) collective-permute-start(bf16[8,128,128]{2,1,0:T(8,128)(2,1)S(1)} %collective-permute-done.18.refs_16_), channel_id=1, source_target_pairs={{2,0},{4,2},{6,4},{7,6},{5,7},{3,5},{1,3},{0,1},{10,8},{12,10},{14... | collective-permute-start | bytes 786440 | tf_op jit(solution)/shard_map/ppermute | solution.py:169
  145.4 1.2 dynamic-slice_bitcast_fusion.source_ref
  147.0 3.7 %collective-permute-done.26.refs_24_ = bf16[8,128,128]{2,1,0:T(8,128)(2,1)} collective-permute-done((bf16[8,128,128]{2,1,0:T(8,128)(2,1)S(1)}, bf16[8,128,128]{2,1,0:T(8,128)(2,1)}, u32[]{:S(2)}, u32[]{:S(2)}) %collective-permute-start.26) | collective-permute-done | bytes 262176 | tf_op jit(solution)/shard_map/ppermute | solution.py:169
  150.8 2.8 %collective-permute-done.12.refs_10_ = bf16[8,128,128]{2,1,0:T(8,128)(2,1)} collective-permute-done((bf16[8,128,128]{2,1,0:T(8,128)(2,1)}, bf16[8,128,128]{2,1,0:T(8,128)(2,1)}, u32[]{:S(2)}, u32[]{:S(2)}) %collective-permute-start.12) | collective-permute-done | bytes 262176 | tf_op jit(solution)/shard_map/ppermute | solution.py:169
  153.7 0.9 copy-done.1
  154.6 29.6 %finish.1 = bf16[32,128,1024]{2,1,0:T(8,128)(2,1)} custom-call(s32[32]{0:T(128)} %fusion.index_ref.row_ref, s32[32]{0:T(128)} %subtract_bitcast_fusion.index_ref.col_ref, s32[2,8]{1,0:T(2,128)} %dynamic-slice_bitcast_fusion.source_ref, bf16[32,128,1024]{2,1,0:T(8,128)(2,1)} %targets_ref.1, bf16[32,128,128]{2,1,0:T(8,128)(2,1)} %bitcast.20, ...), custom_call_target="tpu_custom_call" | custom-call | flops 1207959552 | bytes 16777216 | tf_op jit(solution)/shard_map/finish/pallas_call | solution.py:118
  (89 shorter events, 8.6 us)
Async XLA Ops:
  0.0 38.9 %copy-start = (bf16[32,128,128]{2,1,0:T(8,128)(2,1)S(1)}, bf16[32,128,128]{2,1,0:T(8,128)(2,1)}, u32[]{:S(2)}) copy-start(bf16[32,128,128]{2,1,0:T(8,128)(2,1)} %refs_0_.1) | copy-start | bytes 3145732
  3.0 18.3 %copy-start.4 = (bf16[32,64,128]{2,1,0:T(8,128)(2,1)}, bf16[32,64,128]{2,1,0:T(8,128)(2,1)S(1)}, u32[]{:S(2)}) copy-start(bf16[32,64,128]{2,1,0:T(8,128)(2,1)S(1)} %get-tuple-element.5.refs_0_) | copy-start | bytes 1572868
  3.0 16.2 %collective-permute-start.1 = (bf16[32,64,128]{2,1,0:T(8,128)(2,1)S(1)}, bf16[32,64,128]{2,1,0:T(8,128)(2,1)S(1)}, u32[]{:S(2)}, u32[]{:S(2)}) collective-permute-start(bf16[32,64,128]{2,1,0:T(8,128)(2,1)S(1)} %get-tuple-element.5.refs_0_), channel_id=1, source_target_pairs={{16,0},{24,8},{17,1},{25,9},{18,2},{26,10},{19,3},{27,11},{20,4},{... | collective-permute-start | bytes 1572872 | tf_op jit(solution)/shard_map/ppermute | solution.py:138
  8.0 21.8 %all-to-all-start.1 = ((bf16[8,4,64,128]{3,2,1,0:T(8,128)(2,1)}), bf16[8,4,64,128]{3,2,1,0:T(8,128)(2,1)S(1)}, u32[]{:S(2)}, u32[]{:S(2)}) async-start(bf16[8,4,64,128]{3,2,1,0:T(8,128)(2,1)} %bitcast.21), calls=%async_computation.1 | async-start | bytes 1048576 | tf_op jit(solution)/shard_map/all_to_all | solution.py:177
  15.3 5.1 %collective-permute-start = (bf16[32,64,128]{2,1,0:T(8,128)(2,1)S(1)}, bf16[32,64,128]{2,1,0:T(8,128)(2,1)S(1)}, u32[]{:S(2)}, u32[]{:S(2)}) collective-permute-start(bf16[32,64,128]{2,1,0:T(8,128)(2,1)S(1)} %get-tuple-element.5.refs_0_), channel_id=1, source_target_pairs={{0,8},{8,0},{16,24},{24,16},{1,9},{9,1},{17,25},{25,17},{2,10},{10... | collective-permute-start | bytes 1572872 | tf_op jit(solution)/shard_map/ppermute | solution.py:136
  19.2 2.0 %collective-permute-start.2 = (bf16[32,64,128]{2,1,0:T(8,128)(2,1)S(1)}, bf16[32,64,128]{2,1,0:T(8,128)(2,1)}, u32[]{:S(2)}, u32[]{:S(2)}) collective-permute-start(bf16[32,64,128]{2,1,0:T(8,128)(2,1)S(1)} %collective-permute-done.1.refs_2_), channel_id=1, source_target_pairs={{0,8},{8,0},{16,24},{24,16},{1,9},{9,1},{17,25},{25,17},{2,10},{10... | collective-permute-start | bytes 1572872 | tf_op jit(solution)/shard_map/ppermute | solution.py:139
  29.8 32.1 %copy-start.2 = (bf16[8,4,64,128]{3,2,1,0:T(8,128)(2,1)}, bf16[8,4,64,128]{3,2,1,0:T(8,128)(2,1)S(1)}, u32[]{:S(2)}) copy-start(bf16[8,4,64,128]{3,2,1,0:T(8,128)(2,1)S(1)} %all-to-all-done.1.masked_ref) | copy-start | bytes 1572868
  29.8 32.1 %all-to-all-start = ((bf16[8,4,64,128]{3,2,1,0:T(8,128)(2,1)}), bf16[8,4,64,128]{3,2,1,0:T(8,128)(2,1)S(1)}, u32[]{:S(2)}, u32[]{:S(2)}) async-start(bf16[8,4,64,128]{3,2,1,0:T(8,128)(2,1)} %bitcast.22), calls=%async_computation | async-start | bytes 1048576 | tf_op jit(solution)/shard_map/all_to_all | solution.py:177
  34.7 16.5 %collective-permute-start.27 = (bf16[8,128,128]{2,1,0:T(8,128)(2,1)S(1)}, bf16[8,128,128]{2,1,0:T(8,128)(2,1)S(1)}, u32[]{:S(2)}, u32[]{:S(2)}) collective-permute-start(bf16[8,128,128]{2,1,0:T(8,128)(2,1)S(1)} %get-tuple-element.7), channel_id=1, source_target_pairs={{2,0},{4,2},{6,4},{7,6},{5,7},{3,5},{1,3},{0,1},{10,8},{12,10},{14... | collective-permute-start | bytes 786440 | tf_op jit(solution)/shard_map/ppermute | solution.py:169
  36.8 14.4 %collective-permute-start.20 = (bf16[8,128,128]{2,1,0:T(8,128)(2,1)S(1)}, bf16[8,128,128]{2,1,0:T(8,128)(2,1)}, u32[]{:S(2)}, u32[]{:S(2)}) collective-permute-start(bf16[8,128,128]{2,1,0:T(8,128)(2,1)S(1)} %get-tuple-element.8), channel_id=1, source_target_pairs={{0,2},{2,4},{4,6},{6,7},{7,5},{5,3},{3,1},{1,0},{8,10},{10,12},{12... | collective-permute-start | bytes 786440 | tf_op jit(solution)/shard_map/ppermute | solution.py:169
  36.9 18.9 %collective-permute-start.13 = (bf16[8,128,128]{2,1,0:T(8,128)(2,1)S(1)}, bf16[8,128,128]{2,1,0:T(8,128)(2,1)}, u32[]{:S(2)}, u32[]{:S(2)}) collective-permute-start(bf16[8,128,128]{2,1,0:T(8,128)(2,1)S(1)} %get-tuple-element.9), channel_id=1, source_target_pairs={{2,0},{4,2},{6,4},{7,6},{5,7},{3,5},{1,3},{0,1},{10,8},{12,10},{14... | collective-permute-start | bytes 786440 | tf_op jit(solution)/shard_map/ppermute | solution.py:169
  38.8 22.4 %collective-permute-start.6 = (bf16[8,128,128]{2,1,0:T(8,128)(2,1)S(1)}, bf16[8,128,128]{2,1,0:T(8,128)(2,1)S(1)}, u32[]{:S(2)}, u32[]{:S(2)}) collective-permute-start(bf16[8,128,128]{2,1,0:T(8,128)(2,1)S(1)} %get-tuple-element.10), channel_id=1, source_target_pairs={{0,2},{2,4},{4,6},{6,7},{7,5},{5,3},{3,1},{1,0},{8,10},{10,12},{12... | collective-permute-start | bytes 786440 | tf_op jit(solution)/shard_map/ppermute | solution.py:169
  38.9 74.9 %collective-permute-start.4 = (bf16[32,128,128]{2,1,0:T(8,128)(2,1)S(1)}, bf16[32,128,128]{2,1,0:T(8,128)(2,1)S(1)}, u32[]{:S(2)}, u32[]{:S(2)}) collective-permute-start(bf16[32,128,128]{2,1,0:T(8,128)(2,1)S(1)} %copy-done), channel_id=1, source_target_pairs={{16,0},{24,8},{17,1},{25,9},{18,2},{26,10},{19,3},{27,11},{20,4},{... | collective-permute-start | bytes 3145736 | tf_op jit(solution)/shard_map/ppermute | solution.py:138
  51.2 102.4 %copy-start.8 = (bf16[8,128,128]{2,1,0:T(8,128)(2,1)}, bf16[8,128,128]{2,1,0:T(8,128)(2,1)S(1)}, u32[]{:S(2)}) copy-start(bf16[8,128,128]{2,1,0:T(8,128)(2,1)S(1)} %collective-permute-done.27.refs_25_) | copy-start | bytes 786436
  51.2 70.9 %collective-permute-start.3 = (bf16[32,128,128]{2,1,0:T(8,128)(2,1)S(1)}, bf16[32,128,128]{2,1,0:T(8,128)(2,1)}, u32[]{:S(2)}, u32[]{:S(2)}) collective-permute-start(bf16[32,128,128]{2,1,0:T(8,128)(2,1)S(1)} %copy-done), channel_id=1, source_target_pairs={{0,8},{8,0},{16,24},{24,16},{1,9},{9,1},{17,25},{25,17},{2,10},{10... | collective-permute-start | bytes 3145736 | tf_op jit(solution)/shard_map/ppermute | solution.py:136
  51.2 19.5 %collective-permute-start.28 = (bf16[8,128,128]{2,1,0:T(8,128)(2,1)S(1)}, bf16[8,128,128]{2,1,0:T(8,128)(2,1)}, u32[]{:S(2)}, u32[]{:S(2)}) collective-permute-start(bf16[8,128,128]{2,1,0:T(8,128)(2,1)S(1)} %collective-permute-done.27.refs_25_), channel_id=1, source_target_pairs={{2,0},{4,2},{6,4},{7,6},{5,7},{3,5},{1,3},{0,1},{10,8},{12,10},{14... | collective-permute-start | bytes 786440 | tf_op jit(solution)/shard_map/ppermute | solution.py:169
  55.7 17.1 %collective-permute-start.21 = (bf16[8,128,128]{2,1,0:T(8,128)(2,1)}, bf16[8,128,128]{2,1,0:T(8,128)(2,1)}, u32[]{:S(2)}, u32[]{:S(2)}) collective-permute-start(bf16[8,128,128]{2,1,0:T(8,128)(2,1)} %collective-permute-done.20.refs_18_), channel_id=1, source_target_pairs={{0,2},{2,4},{4,6},{6,7},{7,5},{5,3},{3,1},{1,0},{8,10},{10,12},{12... | collective-permute-start | bytes 786440 | tf_op jit(solution)/shard_map/ppermute | solution.py:169
  61.9 10.9 %collective-permute-start.14 = (bf16[8,128,128]{2,1,0:T(8,128)(2,1)}, bf16[8,128,128]{2,1,0:T(8,128)(2,1)}, u32[]{:S(2)}, u32[]{:S(2)}) collective-permute-start(bf16[8,128,128]{2,1,0:T(8,128)(2,1)} %collective-permute-done.13.refs_11_), channel_id=1, source_target_pairs={{2,0},{4,2},{6,4},{7,6},{5,7},{3,5},{1,3},{0,1},{10,8},{12,10},{14... | collective-permute-start | bytes 786440 | tf_op jit(solution)/shard_map/ppermute | solution.py:169
  67.2 86.4 %all-to-all-start.2 = ((bf16[8,4,128,128]{3,2,1,0:T(8,128)(2,1)}), bf16[8,4,128,128]{3,2,1,0:T(8,128)(2,1)S(1)}, u32[]{:S(2)}, u32[]{:S(2)}) async-start(bf16[8,4,128,128]{3,2,1,0:T(8,128)(2,1)} %broadcast_in_dim.21), calls=%async_computation.2 | async-start | bytes 2097152 | tf_op jit(solution)/shard_map/all_to_all | solution.py:182
  70.8 23.9 %collective-permute-start.7 = (bf16[8,128,128]{2,1,0:T(8,128)(2,1)}, bf16[8,128,128]{2,1,0:T(8,128)(2,1)S(1)}, u32[]{:S(2)}, u32[]{:S(2)}) collective-permute-start(bf16[8,128,128]{2,1,0:T(8,128)(2,1)} %copy-done.9), channel_id=1, source_target_pairs={{0,2},{2,4},{4,6},{6,7},{7,5},{5,3},{3,1},{1,0},{8,10},{10,12},{12... | collective-permute-start | bytes 786440 | tf_op jit(solution)/shard_map/ppermute | solution.py:169
  72.8 23.9 %collective-permute-start.29 = (bf16[8,128,128]{2,1,0:T(8,128)(2,1)}, bf16[8,128,128]{2,1,0:T(8,128)(2,1)S(1)}, u32[]{:S(2)}, u32[]{:S(2)}) collective-permute-start(bf16[8,128,128]{2,1,0:T(8,128)(2,1)} %collective-permute-done.28.refs_26_), channel_id=1, source_target_pairs={{2,0},{4,2},{6,4},{7,6},{5,7},{3,5},{1,3},{0,1},{10,8},{12,10},{14... | collective-permute-start | bytes 786440 | tf_op jit(solution)/shard_map/ppermute | solution.py:169
  72.8 29.1 %collective-permute-start.22 = (bf16[8,128,128]{2,1,0:T(8,128)(2,1)}, bf16[8,128,128]{2,1,0:T(8,128)(2,1)S(1)}, u32[]{:S(2)}, u32[]{:S(2)}) collective-permute-start(bf16[8,128,128]{2,1,0:T(8,128)(2,1)} %collective-permute-done.21.refs_19_), channel_id=1, source_target_pairs={{0,2},{2,4},{4,6},{6,7},{7,5},{5,3},{3,1},{1,0},{8,10},{10,12},{12... | collective-permute-start | bytes 786440 | tf_op jit(solution)/shard_map/ppermute | solution.py:169
  94.6 27.5 %copy-start.10 = (bf16[8,128,128]{2,1,0:T(8,128)(2,1)}, bf16[8,128,128]{2,1,0:T(8,128)(2,1)S(1)}, u32[]{:S(2)}) copy-start(bf16[8,128,128]{2,1,0:T(8,128)(2,1)S(1)} %collective-permute-done.7.refs_5_) | copy-start | bytes 786436
  94.6 11.1 %collective-permute-start.15 = (bf16[8,128,128]{2,1,0:T(8,128)(2,1)}, bf16[8,128,128]{2,1,0:T(8,128)(2,1)S(1)}, u32[]{:S(2)}, u32[]{:S(2)}) collective-permute-start(bf16[8,128,128]{2,1,0:T(8,128)(2,1)} %collective-permute-done.14.refs_12_), channel_id=1, source_target_pairs={{2,0},{4,2},{6,4},{7,6},{5,7},{3,5},{1,3},{0,1},{10,8},{12,10},{14... | collective-permute-start | bytes 786440 | tf_op jit(solution)/shard_map/ppermute | solution.py:169
  96.7 26.3 %copy-start.11 = (bf16[8,128,128]{2,1,0:T(8,128)(2,1)}, bf16[8,128,128]{2,1,0:T(8,128)(2,1)S(1)}, u32[]{:S(2)}) copy-start(bf16[8,128,128]{2,1,0:T(8,128)(2,1)S(1)} %collective-permute-done.29.refs_27_) | copy-start | bytes 786436
  96.7 11.9 %collective-permute-start.8 = (bf16[8,128,128]{2,1,0:T(8,128)(2,1)S(1)}, bf16[8,128,128]{2,1,0:T(8,128)(2,1)S(1)}, u32[]{:S(2)}, u32[]{:S(2)}) collective-permute-start(bf16[8,128,128]{2,1,0:T(8,128)(2,1)S(1)} %collective-permute-done.7.refs_5_), channel_id=1, source_target_pairs={{0,2},{2,4},{4,6},{6,7},{7,5},{5,3},{3,1},{1,0},{8,10},{10,12},{12... | collective-permute-start | bytes 786440 | tf_op jit(solution)/shard_map/ppermute | solution.py:169
  102.0 21.2 %copy-start.12 = (bf16[8,128,128]{2,1,0:T(8,128)(2,1)}, bf16[8,128,128]{2,1,0:T(8,128)(2,1)S(1)}, u32[]{:S(2)}) copy-start(bf16[8,128,128]{2,1,0:T(8,128)(2,1)S(1)} %collective-permute-done.22.refs_20_) | copy-start | bytes 786436
  102.0 9.5 %collective-permute-start.30 = (bf16[8,128,128]{2,1,0:T(8,128)(2,1)S(1)}, bf16[8,128,128]{2,1,0:T(8,128)(2,1)S(1)}, u32[]{:S(2)}, u32[]{:S(2)}) collective-permute-start(bf16[8,128,128]{2,1,0:T(8,128)(2,1)S(1)} %collective-permute-done.29.refs_27_), channel_id=1, source_target_pairs={{2,0},{4,2},{6,4},{7,6},{5,7},{3,5},{1,3},{0,1},{10,8},{12,10},{14... | collective-permute-start | bytes 786440 | tf_op jit(solution)/shard_map/ppermute | solution.py:169
  105.8 21.0 %copy-start.13 = (bf16[8,128,128]{2,1,0:T(8,128)(2,1)}, bf16[8,128,128]{2,1,0:T(8,128)(2,1)S(1)}, u32[]{:S(2)}) copy-start(bf16[8,128,128]{2,1,0:T(8,128)(2,1)S(1)} %collective-permute-done.15.refs_13_) | copy-start | bytes 786436
  105.8 8.4 %collective-permute-start.23 = (bf16[8,128,128]{2,1,0:T(8,128)(2,1)S(1)}, bf16[8,128,128]{2,1,0:T(8,128)(2,1)S(1)}, u32[]{:S(2)}, u32[]{:S(2)}) collective-permute-start(bf16[8,128,128]{2,1,0:T(8,128)(2,1)S(1)} %collective-permute-done.22.refs_20_), channel_id=1, source_target_pairs={{0,2},{2,4},{4,6},{6,7},{7,5},{5,3},{3,1},{1,0},{8,10},{10,12},{12... | collective-permute-start | bytes 786440 | tf_op jit(solution)/shard_map/ppermute | solution.py:169
  108.6 18.2 %copy-start.14 = (bf16[8,128,128]{2,1,0:T(8,128)(2,1)}, bf16[8,128,128]{2,1,0:T(8,128)(2,1)S(1)}, u32[]{:S(2)}) copy-start(bf16[8,128,128]{2,1,0:T(8,128)(2,1)S(1)} %collective-permute-done.8.refs_6_) | copy-start | bytes 786436
  108.6 8.2 %collective-permute-start.16 = (bf16[8,128,128]{2,1,0:T(8,128)(2,1)S(1)}, bf16[8,128,128]{2,1,0:T(8,128)(2,1)S(1)}, u32[]{:S(2)}, u32[]{:S(2)}) collective-permute-start(bf16[8,128,128]{2,1,0:T(8,128)(2,1)S(1)} %collective-permute-done.15.refs_13_), channel_id=1, source_target_pairs={{2,0},{4,2},{6,4},{7,6},{5,7},{3,5},{1,3},{0,1},{10,8},{12,10},{14... | collective-permute-start | bytes 786440 | tf_op jit(solution)/shard_map/ppermute | solution.py:169
  111.5 8.3 %collective-permute-start.9 = (bf16[8,128,128]{2,1,0:T(8,128)(2,1)S(1)}, bf16[8,128,128]{2,1,0:T(8,128)(2,1)S(1)}, u32[]{:S(2)}, u32[]{:S(2)}) collective-permute-start(bf16[8,128,128]{2,1,0:T(8,128)(2,1)S(1)} %collective-permute-done.8.refs_6_), channel_id=1, source_target_pairs={{0,2},{2,4},{4,6},{6,7},{7,5},{5,3},{3,1},{1,0},{8,10},{10,12},{12... | collective-permute-start | bytes 786440 | tf_op jit(solution)/shard_map/ppermute | solution.py:169
  113.8 39.8 %copy-start.5 = (bf16[32,128,128]{2,1,0:T(8,128)(2,1)}, bf16[32,128,128]{2,1,0:T(8,128)(2,1)S(1)}, u32[]{:S(2)}) copy-start(bf16[32,128,128]{2,1,0:T(8,128)(2,1)S(1)} %collective-permute-done.4.refs_2_) | copy-start | bytes 3145732
  113.8 39.8 %collective-permute-start.5 = (bf16[32,128,128]{2,1,0:T(8,128)(2,1)S(1)}, bf16[32,128,128]{2,1,0:T(8,128)(2,1)}, u32[]{:S(2)}, u32[]{:S(2)}) collective-permute-start(bf16[32,128,128]{2,1,0:T(8,128)(2,1)S(1)} %collective-permute-done.4.refs_2_), channel_id=1, source_target_pairs={{0,8},{8,0},{16,24},{24,16},{1,9},{9,1},{17,25},{25,17},{2,10},{10... | collective-permute-start | bytes 3145736 | tf_op jit(solution)/shard_map/ppermute | solution.py:139
  114.2 9.0 %collective-permute-start.31 = (bf16[8,128,128]{2,1,0:T(8,128)(2,1)S(1)}, bf16[8,128,128]{2,1,0:T(8,128)(2,1)S(1)}, u32[]{:S(2)}, u32[]{:S(2)}) collective-permute-start(bf16[8,128,128]{2,1,0:T(8,128)(2,1)S(1)} %collective-permute-done.30.refs_28_), channel_id=1, source_target_pairs={{2,0},{4,2},{6,4},{7,6},{5,7},{3,5},{1,3},{0,1},{10,8},{12,10},{14... | collective-permute-start | bytes 786440 | tf_op jit(solution)/shard_map/ppermute | solution.py:169
  116.8 9.9 %collective-permute-start.24 = (bf16[8,128,128]{2,1,0:T(8,128)(2,1)S(1)}, bf16[8,128,128]{2,1,0:T(8,128)(2,1)S(1)}, u32[]{:S(2)}, u32[]{:S(2)}) collective-permute-start(bf16[8,128,128]{2,1,0:T(8,128)(2,1)S(1)} %collective-permute-done.23.refs_21_), channel_id=1, source_target_pairs={{0,2},{2,4},{4,6},{6,7},{7,5},{5,3},{3,1},{1,0},{8,10},{10,12},{12... | collective-permute-start | bytes 786440 | tf_op jit(solution)/shard_map/ppermute | solution.py:169
  119.8 10.2 %collective-permute-start.17 = (bf16[8,128,128]{2,1,0:T(8,128)(2,1)S(1)}, bf16[8,128,128]{2,1,0:T(8,128)(2,1)S(1)}, u32[]{:S(2)}, u32[]{:S(2)}) collective-permute-start(bf16[8,128,128]{2,1,0:T(8,128)(2,1)S(1)} %collective-permute-done.16.refs_14_), channel_id=1, source_target_pairs={{2,0},{4,2},{6,4},{7,6},{5,7},{3,5},{1,3},{0,1},{10,8},{12,10},{14... | collective-permute-start | bytes 786440 | tf_op jit(solution)/shard_map/ppermute | solution.py:169
  122.1 11.7 %collective-permute-start.10 = (bf16[8,128,128]{2,1,0:T(8,128)(2,1)S(1)}, bf16[8,128,128]{2,1,0:T(8,128)(2,1)S(1)}, u32[]{:S(2)}, u32[]{:S(2)}) collective-permute-start(bf16[8,128,128]{2,1,0:T(8,128)(2,1)S(1)} %collective-permute-done.9.refs_7_), channel_id=1, source_target_pairs={{0,2},{2,4},{4,6},{6,7},{7,5},{5,3},{3,1},{1,0},{8,10},{10,12},{12... | collective-permute-start | bytes 786440 | tf_op jit(solution)/shard_map/ppermute | solution.py:169
  123.2 12.5 %collective-permute-start.32 = (bf16[8,128,128]{2,1,0:T(8,128)(2,1)S(1)}, bf16[8,128,128]{2,1,0:T(8,128)(2,1)S(1)}, u32[]{:S(2)}, u32[]{:S(2)}) collective-permute-start(bf16[8,128,128]{2,1,0:T(8,128)(2,1)S(1)} %collective-permute-done.31.refs_29_), channel_id=1, source_target_pairs={{2,0},{4,2},{6,4},{7,6},{5,7},{3,5},{1,3},{0,1},{10,8},{12,10},{14... | collective-permute-start | bytes 786440 | tf_op jit(solution)/shard_map/ppermute | solution.py:169
  126.8 12.7 %collective-permute-start.25 = (bf16[8,128,128]{2,1,0:T(8,128)(2,1)S(1)}, bf16[8,128,128]{2,1,0:T(8,128)(2,1)S(1)}, u32[]{:S(2)}, u32[]{:S(2)}) collective-permute-start(bf16[8,128,128]{2,1,0:T(8,128)(2,1)S(1)} %collective-permute-done.24.refs_22_), channel_id=1, source_target_pairs={{0,2},{2,4},{4,6},{6,7},{7,5},{5,3},{3,1},{1,0},{8,10},{10,12},{12... | collective-permute-start | bytes 786440 | tf_op jit(solution)/shard_map/ppermute | solution.py:169
  130.1 11.2 %collective-permute-start.18 = (bf16[8,128,128]{2,1,0:T(8,128)(2,1)S(1)}, bf16[8,128,128]{2,1,0:T(8,128)(2,1)S(1)}, u32[]{:S(2)}, u32[]{:S(2)}) collective-permute-start(bf16[8,128,128]{2,1,0:T(8,128)(2,1)S(1)} %collective-permute-done.17.refs_15_), channel_id=1, source_target_pairs={{2,0},{4,2},{6,4},{7,6},{5,7},{3,5},{1,3},{0,1},{10,8},{12,10},{14... | collective-permute-start | bytes 786440 | tf_op jit(solution)/shard_map/ppermute | solution.py:169
  133.8 19.8 %copy-start.22 = (bf16[8,128,128]{2,1,0:T(8,128)(2,1)}, bf16[8,128,128]{2,1,0:T(8,128)(2,1)S(1)}, u32[]{:S(2)}) copy-start(bf16[8,128,128]{2,1,0:T(8,128)(2,1)S(1)} %collective-permute-done.10.refs_8_) | copy-start | bytes 786436
  133.8 11.3 %collective-permute-start.11 = (bf16[8,128,128]{2,1,0:T(8,128)(2,1)S(1)}, bf16[8,128,128]{2,1,0:T(8,128)(2,1)}, u32[]{:S(2)}, u32[]{:S(2)}) collective-permute-start(bf16[8,128,128]{2,1,0:T(8,128)(2,1)S(1)} %collective-permute-done.10.refs_8_), channel_id=1, source_target_pairs={{0,2},{2,4},{4,6},{6,7},{7,5},{5,3},{3,1},{1,0},{8,10},{10,12},{12... | collective-permute-start | bytes 786440 | tf_op jit(solution)/shard_map/ppermute | solution.py:169
  135.7 11.3 %collective-permute-start.33 = (bf16[8,128,128]{2,1,0:T(8,128)(2,1)S(1)}, bf16[8,128,128]{2,1,0:T(8,128)(2,1)}, u32[]{:S(2)}, u32[]{:S(2)}) collective-permute-start(bf16[8,128,128]{2,1,0:T(8,128)(2,1)S(1)} %collective-permute-done.32.refs_30_), channel_id=1, source_target_pairs={{2,0},{4,2},{6,4},{7,6},{5,7},{3,5},{1,3},{0,1},{10,8},{12,10},{14... | collective-permute-start | bytes 786440 | tf_op jit(solution)/shard_map/ppermute | solution.py:169
  139.4 11.3 %collective-permute-start.26 = (bf16[8,128,128]{2,1,0:T(8,128)(2,1)S(1)}, bf16[8,128,128]{2,1,0:T(8,128)(2,1)}, u32[]{:S(2)}, u32[]{:S(2)}) collective-permute-start(bf16[8,128,128]{2,1,0:T(8,128)(2,1)S(1)} %collective-permute-done.25.refs_23_), channel_id=1, source_target_pairs={{0,2},{2,4},{4,6},{6,7},{7,5},{5,3},{3,1},{1,0},{8,10},{10,12},{12... | collective-permute-start | bytes 786440 | tf_op jit(solution)/shard_map/ppermute | solution.py:169
  141.3 9.5 %collective-permute-start.19 = (bf16[8,128,128]{2,1,0:T(8,128)(2,1)S(1)}, bf16[8,128,128]{2,1,0:T(8,128)(2,1)}, u32[]{:S(2)}, u32[]{:S(2)}) collective-permute-start(bf16[8,128,128]{2,1,0:T(8,128)(2,1)S(1)} %collective-permute-done.18.refs_16_), channel_id=1, source_target_pairs={{2,0},{4,2},{6,4},{7,6},{5,7},{3,5},{1,3},{0,1},{10,8},{12,10},{14... | collective-permute-start | bytes 786440 | tf_op jit(solution)/shard_map/ppermute | solution.py:169
  145.2 8.4 %collective-permute-start.12 = (bf16[8,128,128]{2,1,0:T(8,128)(2,1)}, bf16[8,128,128]{2,1,0:T(8,128)(2,1)}, u32[]{:S(2)}, u32[]{:S(2)}) collective-permute-start(bf16[8,128,128]{2,1,0:T(8,128)(2,1)} %collective-permute-done.11.refs_9_), channel_id=1, source_target_pairs={{0,2},{2,4},{4,6},{6,7},{7,5},{5,3},{3,1},{1,0},{8,10},{10,12},{12... | collective-permute-start | bytes 786440 | tf_op jit(solution)/shard_map/ppermute | solution.py:169
  (15 other events, 142.5 us)
